TPU v7x, 32 devices: a whole 2x2x4 slice. The times are simulated.
32 devices in a mesh: dp: 4 (over y, core), vocab: 8 (over z, x).
Axes of the slice: x: 2, y: 2, z: 4, core: 2. Of those that a mesh axis runs over, the one named last changes fastest.
Arguments:
- hidden: bfloat16 [256, 3584], P('dp'), may hold values from -48 to 48
- embedding: bfloat16 [24576, 3584], P(('dp', 'vocab')), may hold values from -1 to 1
- targets: int32 [256], P('dp'), may hold values from 0 to 24575
- loss_weight: bfloat16 [256], P('dp'), may hold values from 1 to 10
Outputs:
- hidden_grad: bfloat16 [256, 3584], P('dp')
- table_grad: bfloat16 [24576, 3584], P(('dp', 'vocab'))
All inputs are finite; a program needn't handle non-finite values.
Results may differ from a plain program's by a relative error of at most 0.0049.
Values may be sent and summed in bfloat16 or wider, within the bound.
A program may use at most 128 MiB of HBM per device.

v0:
```python
import jax
import jax.numpy as jnp
from jax import lax
from jax.sharding import PartitionSpec as P

soft_cap = 30.0
z_weight = 0.002


def body(hidden, embedding, targets, loss_weight):
    shard_rows = embedding.shape[0]
    group_hidden, group_weight = (
        lax.all_gather(hidden, "dp", axis=0, tiled=True),
        lax.all_gather(loss_weight, "dp", axis=0, tiled=True),
    )
    group_targets = lax.all_gather(targets, "dp", axis=0, tiled=True)
    logits = lax.dot_general(
        group_hidden, embedding, (((1,), (1,)), ((), ())), preferred_element_type=jnp.float32
    )
    capped = soft_cap * jnp.tanh(logits / soft_cap)
    exp_terms = jnp.exp(capped - soft_cap)
    partial_value = jnp.sum(exp_terms, axis=1)
    weight = group_weight.astype(jnp.float32)
    device_place = lax.axis_index("dp") * lax.axis_size("vocab") + lax.axis_index("vocab")
    exp_total = lax.psum(partial_value, ("dp", "vocab"))
    factor = weight * (1.0 + 2.0 * z_weight * (soft_cap + jnp.log(exp_total))) / exp_total
    columns = device_place * shard_rows + lax.iota(jnp.int32, shard_rows)
    target_hit = group_targets[:, None] == columns[None, :]
    softmax_part = factor[:, None] * exp_terms - jnp.where(target_hit, weight[:, None], 0.0)
    scores_grad = (softmax_part * (1.0 - (capped / soft_cap) ** 2)).astype(jnp.bfloat16)
    table_grad = lax.dot_general(
        scores_grad, group_hidden, (((0,), (0,)), ((), ())), preferred_element_type=jnp.float32
    ).astype(jnp.bfloat16)
    group_grad = lax.psum_scatter(
        jnp.dot(scores_grad, embedding, preferred_element_type=jnp.float32),
        "dp",
        scatter_dimension=0,
        tiled=True,
    )
    hidden_grad = lax.psum(group_grad, "vocab").astype(jnp.bfloat16)
    return (hidden_grad, table_grad)


def solution(mesh):
    return jax.shard_map(
        body,
        mesh=mesh,
        in_specs=(P("dp", None), P(("dp", "vocab"), None), P("dp"), P("dp")),
        out_specs=(P("dp", None), P(("dp", "vocab"), None)),
        check_vma=False,
    )
```

profile of v0, /device:TPU:0, one launch (start us, length us, event | category | flops | bytes accessed | tf_op | source)
XLA Modules:
  0.0 182.5 jit_solution(10813239611045289594)
XLA Ops:
  7.2 0.0 all-gather.2.cloned.1.call-start
  7.2 0.7 all-gather.2.cloned.1.call-update
  7.9 0.0 reduce-scatter.2.cloned.1.call-start
  8.0 1.2 dynamic-slice
  9.9 0.9 dynamic-update-slice
  10.7 8.4 %all-reduce = bf16[256]{0:T(256)(128)(2,1)S(1)} all-reduce(bf16[256]{0:T(256)(128)(2,1)S(1)} %dynamic-update-slice), channel_id=1, replica_groups=mesh['dp'=4,'vocab'=8] {'dp'}, use_global_device_ids=true, to_apply=%add | all-reduce | flops 256 | bytes 1024
  19.1 0.9 dynamic-update-slice.1
  20.0 4.5 %all-reduce.1 = s32[256]{0:T(256)S(1)} all-reduce(s32[256]{0:T(256)S(1)} %dynamic-update-slice.1), channel_id=1, replica_groups=mesh['dp'=4,'vocab'=8] {'dp'}, use_global_device_ids=true, to_apply=%add.1 | all-reduce | flops 256 | bytes 2048
  24.4 9.0 %all-gather.2.cloned.1.call-done = bf16[256,3584]{1,0:T(8,128)(2,1)} async-done(((bf16[64,3584]{1,0:T(8,128)(2,1)}), bf16[256,3584]{1,0:T(8,128)(2,1)}) %all-gather.2.cloned.1.call-update) | async-done | bytes 1835024 | tf_op jit(solution)/shard_map/all_gather | solution.py:13
  33.5 4.9 %fusion.1 = (f32[256]{0:T(256)S(1)}, f32[256,768]{1,0:T(8,128)S(1)}) fusion(bf16[256,3584]{1,0:T(8,128)(2,1)} %all-gather.2.cloned.1.call-done, bf16[768,3584]{1,0:T(8,128)(2,1)} %param.5), kind=kOutput, calls=%fused_computation.5 | convolution fusion | flops 1410072320 | bytes 8127488 | tf_op jit(solution)/shard_map/dot_general | solution.py:17
  38.4 39.3 %psum.14 = f32[256]{0:T(256)S(1)} all-reduce(f32[256]{0:T(256)S(1)} %get-tuple-element.2), channel_id=1, replica_groups=mesh['dp'=4,'vocab'=8] {'dp','vocab'}, use_global_device_ids=true, to_apply=%region_1.0 | all-reduce | flops 256 | bytes 2048 | tf_op jit(solution)/shard_map/psum | solution.py:25
  77.7 0.0 copy-start
  77.7 6.3 %fusion.2 = f32[256,3584]{1,0:T(8,128)} fusion(bf16[768,3584]{1,0:T(8,128)(2,1)} %param.5, f32[256,768]{1,0:T(8,128)S(1)} %get-tuple-element.3, f32[256]{0:T(256)S(1)} %convert_element_type.12, s32[768]{0:T(1024)S(1)} %iota_add_fusion, f32[256]{0:T(256)S(1)} %multiply_divide_fusion, s32[256]{0:T(256)S(1)} %all-reduce.1), kind=kOutput, calls=%fused_computation.8 | convolution fusion | flops 1411252224 | bytes 9967616 | tf_op jit(solution)/shard_map/dot_general | solution.py:35
  84.0 0.0 reduce-scatter.2.cloned.1.call-update
  84.0 0.0 copy-done
  84.0 4.3 %convolution_convert_fusion = bf16[768,3584]{1,0:T(8,128)(2,1)} fusion(bf16[256,3584]{1,0:T(8,128)(2,1)S(1)} %copy-done, f32[256,768]{1,0:T(8,128)S(1)} %get-tuple-element.3, f32[256]{0:T(256)S(1)} %convert_element_type.12, s32[768]{0:T(1024)S(1)} %iota_add_fusion, f32[256]{0:T(256)S(1)} %multiply_divide_fusion, s32[256]{0:T(256)S(1)} %all-reduce.1), kind=kOutput, calls=%fused_computation | convolution fusion | flops 1414004736 | bytes 8132608 | tf_op jit(solution)/shard_map/dot_general | solution.py:31
  88.3 37.9 %reduce-scatter.2.cloned.1.call-done = f32[64,3584]{1,0:T(8,128)} async-done(((f32[256,3584]{1,0:T(8,128)}), f32[64,3584]{1,0:T(8,128)}) %reduce-scatter.2.cloned.1.call-update) | async-done | bytes 917520 | tf_op jit(solution)/shard_map/reduce_scatter | solution.py:34
  126.2 49.4 %all-reduce.3 = bf16[64,3584]{1,0:T(8,128)(2,1)} all-reduce(f32[64,3584]{1,0:T(8,128)} %reduce-scatter.2.cloned.1.call-done), channel_id=1, replica_groups=mesh['dp'=4,'vocab'=8] {'vocab'}, use_global_device_ids=true, to_apply=%region_3.4 | all-reduce | flops 229376 | bytes 1376256 | tf_op jit(solution)/shard_map/psum | solution.py:40
  (5 shorter events, 0.0 us)
Async XLA Ops:
  7.2 26.3 %all-gather.2.cloned.1.call-start = ((), (), s32[]{:S(2)}) async-start(), calls=%async_computation.1 | async-start | bytes 2293760 | tf_op jit(solution)/shard_map/all_gather | solution.py:13
  7.9 118.3 %reduce-scatter.2.cloned.1.call-start = ((), (), s32[]{:S(2)}) async-start(), calls=%async_computation.2 | async-start | bytes 4587520 | tf_op jit(solution)/shard_map/reduce_scatter | solution.py:34
  77.7 6.3 %copy-start = (bf16[256,3584]{1,0:T(8,128)(2,1)S(1)}, bf16[256,3584]{1,0:T(8,128)(2,1)}, u32[]{:S(2)}) copy-start(bf16[256,3584]{1,0:T(8,128)(2,1)} %all-gather.2.cloned.1.call-done) | copy-start | bytes 5505028
Sparse Core Ops, SparseCore 0:
  9.5 23.9 all-gather.1
  84.1 42.0 reduce-scatter.1
where the time goes:
time: 183 us; the launch traced here: 182 us
  blocking collectives  102 us (56%)
  waiting for transfers between devices  47.6 us (26%)
  matrix products  15.4 us (8%)
  between operations  14.7 us (8%)
  local copies, waits for them, and re-layouts  2.97 us (2%)
    psum x1, blocking collectives, body(): hidden_grad = lax.psum(group_grad, 'vocab').astype(jnp.bfloat16)  49.4 us
    psum x1, blocking collectives, body(): exp_total = lax.psum(partial_value, ('dp', 'vocab'))  39.3 us
    reduce_scatter x1, waiting for transfers between devices, body(): lax.psum_scatter(jnp.dot(scores_grad, embedding, preferred_element_type=j...  37.9 us
    unnamed x2, blocking collectives  12.8 us
    all_gather x1, waiting for transfers between devices, body(): lax.all_gather(hidden, 'dp', axis=0, tiled=True)  9.04 us
    dot_general x1, matrix products, body(): jnp.dot(scores_grad, embedding, preferred_element_type=jnp.float32)  6.28 us
    dot_general x1, matrix products, body(): lax.dot_general(group_hidden, embedding, (((1,), (1,)), ((), ())), prefer...  4.91 us
    dot_general x1, matrix products, body(): lax.dot_general(scores_grad, group_hidden, (((0,), (0,)), ((), ())), pref...  4.26 us
  transfers between devices with their start and end apart: 2, of which 2 were waited for; matrix products, arithmetic and copies ran while one was open for 4% of the time, Pallas kernels for 0%

commit v1 on v0

v1 whole, which is shorter than its diff:
```python
import functools

import jax
import jax.numpy as jnp
from jax import lax
from jax.experimental import pallas as pl
from jax.experimental.pallas import tpu as pltpu
from jax.sharding import PartitionSpec as P

soft_cap = 30.0
z_weight = 0.002
MESH = pl.DeviceIdType.MESH
f32, bf16 = jnp.float32, jnp.bfloat16


def kernel(cfg, hidden, embedding, marks, hgrad, tgrad,
           hid, emb, tw, pd, pv, uT, eT, sT, sN, gF, sC, rC, sY, rY, bF, sX, rX, sZ, rZ, out, tg,
           loc, tw_s, tw_r, hc_s, hc_r, hy_s, hy_r, hf_s, hf_r, pd_s, pd_r, pv_s, pv_r,
           c_s, c_r, y_s, y_r, x_s, x_r, z_s, z_r, az_s, az_r, ax_s, ax_r, tg_s):
    nd, nv, full, ck, AQ, VB = cfg
    Y, Z = nd // 2, nv // 2
    rows, D = hidden.shape
    V = embedding.shape[0]
    K = D // ck
    G8 = rows // 8
    d, v = lax.axis_index("dp"), lax.axis_index("vocab")
    c, y = lax.rem(d, 2), d // 2
    x, z = lax.rem(v, 2), v // 2
    dev = lambda dd, vv: dict(device_id=(dd, vv), device_id_type=MESH)
    core = dev(y * 2 + 1 - c, v)
    xdev = dev(d, z * 2 + 1 - x)
    ydev = lambda k: dev(lax.rem(y + k, Y) * 2 + c, v)
    zdev = lambda k: dev(d, lax.rem(z + k, Z) * 2 + x)
    rdma = lambda s, t, ss, rs, dv: pltpu.make_async_remote_copy(src_ref=s, dst_ref=t, send_sem=ss, recv_sem=rs, **dv)

    own = pl.ds(pl.multiple_of(d * rows, rows), rows)
    load_h = pltpu.make_async_copy(hidden, hid.at[own], loc.at[0])
    load_h.start()
    load_e = pltpu.make_async_copy(embedding, emb, loc.at[1])
    load_e.start()
    barrier = pltpu.get_barrier_semaphore()
    for k in range(1, nd):
        pl.semaphore_signal(barrier, inc=1, **dev(lax.rem(d + k, nd), v))
    for k in range(1, nv):
        pl.semaphore_signal(barrier, inc=1, **dev(d, lax.rem(v + k, nv)))
    tw[0] = marks[...]
    load_h.wait()
    pl.semaphore_wait(barrier, nd + nv - 2)

    sends = []

    def go(copy):
        copy.start()
        sends.append(copy)
        return copy

    aq = rows // AQ
    part = lambda dd, q: pl.ds(pl.multiple_of(dd * rows + q * aq, aq), aq)
    hy = lambda k, q: rdma(hid.at[part(d, q)], hid.at[part(d, q)], hy_s.at[k - 1, q], hy_r.at[k - 1, q], ydev(k))
    for q in range(AQ):
        for k in range(1, Y):
            go(hy(k, q))
    hc = go(rdma(hid.at[own], hid.at[own], hc_s.at[0], hc_r.at[0], core))
    tws = [go(rdma(tw.at[0], tw.at[k], tw_s.at[k - 1], tw_r.at[k - 1], dev(lax.rem(d + k, nd), v))) for k in range(1, nd)]
    forwards = []
    for q in range(AQ):
        for k in range(1, Y):
            hy(k, q).wait_recv()
            src = lax.rem(y + Y - k, Y) * 2 + c
            forwards.append(go(rdma(hid.at[part(src, q)], hid.at[part(src, q)], hf_s.at[k - 1, q], hf_r.at[k - 1, q], core)))
    hc.wait_recv()
    for copy in tws:
        copy.wait_recv()
    for copy in forwards:
        copy.wait_recv()
    load_e.wait()

    T = hid.shape[0]
    pd[0] = jnp.zeros_like(pd[0])

    def logits_block(b, carry):
        vb = pl.ds(pl.multiple_of(b * VB, VB), VB)
        lg = lax.dot_general(emb[vb, :], hid[...], (((1,), (1,)), ((), ())), preferred_element_type=f32)
        u = jnp.tanh(lg * (1.0 / soft_cap))
        e = jnp.exp(soft_cap * u - soft_cap)
        uT[vb, :] = 1.0 - u * u
        eT[vb, :] = e
        pd[0] += jnp.sum(e.reshape(VB // 8, 8, T), axis=0)
        return carry

    lax.fori_loop(0, V // VB, logits_block, 0)

    pds = [go(rdma(pd.at[0], pd.at[k], pd_s.at[k - 1], pd_r.at[k - 1], dev(lax.rem(d + k, nd), v))) for k in range(1, nd)]
    for copy in pds:
        copy.wait_recv()
    pv[0] = jnp.sum(pd[...], axis=0)
    pvs = [go(rdma(pv.at[0], pv.at[k], pv_s.at[k - 1], pv_r.at[k - 1], dev(d, lax.rem(v + k, nv)))) for k in range(1, nv)]
    for copy in pvs:
        copy.wait_recv()
    total = jnp.sum(jnp.sum(pv[...], axis=0), axis=0, keepdims=True)
    group = jnp.sum(tw[...], axis=0)
    weight, target = group[0:1, :], group[1:2, :]
    factor = weight * (1.0 + 2.0 * z_weight * (soft_cap + jnp.log(total))) / total
    first = (d * nv + v) * V

    def scores_block(b, carry):
        vb = pl.ds(pl.multiple_of(b * VB, VB), VB)
        cols = (first + b * VB + lax.broadcasted_iota(jnp.int32, (VB, T), 0)).astype(f32)
        s = (factor * eT[vb, :] - jnp.where(cols == target, weight, 0.0)) * uT[vb, :]
        sT[vb, :] = s.astype(bf16)
        sN[:, vb] = s.T.astype(bf16)
        return carry

    lax.fori_loop(0, V // VB, scores_block, 0)

    ccopy = lambda j: rdma(sC.at[j], rC.at[j], c_s.at[j], c_r.at[j], core)

    def grad_block(j, carry):
        g = jnp.dot(sN[...], emb[:, pl.ds(pl.multiple_of(j * ck, ck), ck)], preferred_element_type=f32)
        gF[j] = g.reshape(nd, rows, ck)
        for yy in range(Y):
            sC[j, yy] = gF[j, yy * 2 + 1 - c].astype(bf16)
        ccopy(j).start()
        return carry

    lax.fori_loop(0, K, grad_block, 0)
    ycopy = lambda j, k: rdma(sY.at[j, k - 1], rY.at[j, k - 1], y_s.at[j, k - 1], y_r.at[j, k - 1], ydev(k))

    def core_block(j, carry):
        ccopy(j).wait()
        for k in range(1, Y):
            yy = lax.rem(y + k, Y)
            sY[j, k - 1] = (gF[j, yy * 2 + c] + rC[j, yy].astype(f32)).astype(bf16)
            ycopy(j, k).start()
        return carry

    lax.fori_loop(0, K, core_block, 0)

    VT = V // VB
    tcopy = lambda b: pltpu.make_async_copy(tg.at[b], tgrad.at[pl.ds(pl.multiple_of(b * VB, VB), VB)], tg_s.at[b])

    def table_block(b, carry):
        vb = pl.ds(pl.multiple_of(b * VB, VB), VB)
        for j in range(K):
            cs = pl.ds(j * ck, ck)
            tg[b, :, cs] = jnp.dot(sT[vb, :], hid[:, cs], preferred_element_type=f32).astype(bf16)
        tcopy(b).start()
        return carry

    lax.fori_loop(0, VT, table_block, 0)

    def y_block(j):
        acc = gF[j, y * 2 + c] + rC[j, y].astype(f32)
        for k in range(1, Y):
            ycopy(j, k).wait()
            acc = acc + rY[j, k - 1].astype(f32)
        return acc

    if not full:
        for j in range(K):
            hgrad[:, j * ck:(j + 1) * ck] = y_block(j)
    else:
        h = G8 // 2
        gz = h // Z
        xcopy = lambda j: rdma(sX.at[j], rX.at[j], x_s.at[j], x_r.at[j], xdev)
        zcopy = lambda j, k: rdma(sZ.at[j, k - 1], rZ.at[j, k - 1], z_s.at[j, k - 1], z_r.at[j, k - 1], zdev(k))
        mine = lambda j: out.at[pl.ds(x * h + z * gz, gz), :, pl.ds(j * ck, ck)]
        half = lambda j: out.at[pl.ds(x * h, h), :, pl.ds(j * ck, ck)]
        azcopy = lambda j, k: rdma(mine(j), mine(j), az_s.at[j, k - 1], az_r.at[j, k - 1], zdev(k))
        axcopy = lambda j: rdma(half(j), half(j), ax_s.at[j], ax_r.at[j], xdev)
        xsum = lambda j, zz: bF[j, pl.ds(x * h + zz * gz, gz)] + rX[j, pl.ds(zz * gz, gz)].astype(f32)

        def stage0(j):
            bF[j] = y_block(j).reshape(G8, 8, ck)
            sX[j] = bF[j, pl.ds((1 - x) * h, h)].astype(bf16)
            xcopy(j).start()

        def stage1(j):
            xcopy(j).wait()
            for k in range(1, Z):
                sZ[j, k - 1] = xsum(j, lax.rem(z + k, Z)).astype(bf16)
                zcopy(j, k).start()

        def stage2(j):
            acc = xsum(j, z)
            for k in range(1, Z):
                zcopy(j, k).wait()
                acc = acc + rZ[j, k - 1].astype(f32)
            out[pl.ds(x * h + z * gz, gz), :, pl.ds(j * ck, ck)] = acc.astype(bf16)
            for k in range(1, Z):
                azcopy(j, k).start()

        def stage3(j):
            for k in range(1, Z):
                azcopy(j, k).wait()
            axcopy(j).start()

        def stage4(j):
            axcopy(j).wait()

        stages = [stage0, stage1, stage2, stage3, stage4]
        for s in range(K + len(stages) - 1):
            for i, stage in enumerate(stages):
                if 0 <= s - i < K:
                    stage(s - i)
        hgrad[...] = out[...]
    for b in range(VT):
        tcopy(b).wait()
    for copy in sends:
        copy.wait_send()


def body(hidden, embedding, targets, loss_weight):
    nd, nv = lax.axis_size("dp"), lax.axis_size("vocab")
    rows, D = hidden.shape
    V = embedding.shape[0]
    T = rows * nd
    Y, Z = nd // 2, nv // 2
    ck = next(s for s in (512, 256, 128, D) if D % s == 0)
    K = D // ck
    AQ = 2
    VB = next(s for s in (256, 128, V) if V % s == 0)
    G8 = rows // 8
    full = G8 % nv == 0
    d = lax.axis_index("dp")
    here = (lax.iota(jnp.int32, T) // rows == d)[None, :]
    line = jnp.stack([loss_weight.astype(f32), targets.astype(f32)])
    marks = jnp.pad(jnp.where(here, jnp.tile(line, (1, nd)), 0.0), ((0, 6), (0, 0)))
    h = G8 // 2
    gz = max(h // Z, 1)
    Zs, Ys = max(Z - 1, 1), max(Y - 1, 1)
    VM = pltpu.VMEM
    dma = lambda *shape: pltpu.SemaphoreType.DMA(shape)
    scratch = [
        VM((T, D), bf16), VM((V, D), bf16), VM((nd, 8, T), f32), VM((nd, 8, T), f32), VM((nv, 8, T), f32),
        VM((V, T), f32), VM((V, T), f32), VM((V, T), bf16), VM((T, V), bf16),
        VM((K, nd, rows, ck), f32), VM((K, Y, rows, ck), bf16), VM((K, Y, rows, ck), bf16),
        VM((K, Ys, rows, ck), bf16), VM((K, Ys, rows, ck), bf16),
        VM((K, G8, 8, ck), f32), VM((K, h, 8, ck), bf16), VM((K, h, 8, ck), bf16),
        VM((K, Zs, gz, 8, ck), bf16), VM((K, Zs, gz, 8, ck), bf16),
        VM((G8, 8, D), bf16), VM((V // VB, VB, D), bf16),
        dma(2), dma(nd), dma(nd), dma(1), dma(1), dma(Ys, AQ), dma(Ys, AQ), dma(Ys, AQ), dma(Ys, AQ),
        dma(nd), dma(nd), dma(nv), dma(nv),
        dma(K), dma(K), dma(K, Ys), dma(K, Ys), dma(K), dma(K), dma(K, Zs), dma(K, Zs), dma(K, Zs), dma(K, Zs), dma(K), dma(K),
        dma(V // VB),
    ]
    hshape = jax.ShapeDtypeStruct((G8, 8, D), bf16) if full else jax.ShapeDtypeStruct((rows, D), f32)
    any_spec = pl.BlockSpec(memory_space=pl.ANY)
    vmem_spec = pl.BlockSpec(memory_space=pltpu.VMEM)
    hgrad, tgrad = pl.pallas_call(
        functools.partial(kernel, (nd, nv, full, ck, AQ, VB)),
        out_shape=(hshape, jax.ShapeDtypeStruct((V, D), bf16)),
        in_specs=[any_spec, any_spec, vmem_spec],
        out_specs=(vmem_spec, any_spec),
        scratch_shapes=scratch,
        compiler_params=pltpu.CompilerParams(collective_id=0, has_side_effects=True, vmem_limit_bytes=60 * 1024 * 1024),
    )(hidden, embedding, marks)
    if full:
        return hgrad.reshape(rows, D), tgrad
    return lax.psum(hgrad, "vocab").astype(bf16), tgrad


def solution(mesh):
    return jax.shard_map(
        body,
        mesh=mesh,
        in_specs=(P("dp", None), P(("dp", "vocab"), None), P("dp"), P("dp")),
        out_specs=(P("dp", None), P(("dp", "vocab"), None)),
        check_vma=False,
    )
```

time: 183 us -> 76.2 us (0.42)
  blocking collectives: 102 us -> 0 us
  Pallas kernels: 0 us -> 66.1 us
  waiting for transfers between devices: 47.6 us -> 0 us
  matrix products: 15.4 us -> 0 us
  between operations: 14.7 us -> 0.65 us
  local copies, waits for them, and re-layouts: 2.97 us -> 7.87 us
    psum x2 -> x0, blocking collectives: 88.7 us -> none  [the longest x1 49.4 us: body(): hidden_grad = lax.psum(group_grad, 'vocab').astype(jnp.bfloat16)]
    pallas_call x0 -> x1, Pallas kernels: none -> 66.1 us  [body(): pl.pallas_call(functools.partial(kernel, (nd, nv, full, ck, AQ, VB)), out...]
    reduce_scatter x1 -> x0, waiting for transfers between devices: 37.9 us -> none  [body(): lax.psum_scatter(jnp.dot(scores_grad, embedding, preferred_element_type=j...]
    dot_general x3 -> x0, matrix products: 15.4 us -> none  [the longest x1 6.28 us: body(): jnp.dot(scores_grad, embedding, preferred_element_type=jnp.float32)]
    unnamed x2 -> x0, blocking collectives: 12.8 us -> none
    all_gather x1 -> x0, waiting for transfers between devices: 9.04 us -> none  [body(): lax.all_gather(hidden, 'dp', axis=0, tiled=True)]
    unnamed x7 -> x2, local copies, waits for them, and re-layouts: 2.97 us -> 7.17 us
  transfers between devices with their start and end apart: 2 -> 0, of which waited for: 2 -> 0; matrix products, arithmetic and copies ran while one was open for 4% -> 0% of each run, Pallas kernels for 0% -> 0%
where the time goes in v1:
time: 76.2 us; the launch traced here: 76 us
  Pallas kernels  66.1 us (87%)
  local copies, waits for them, and re-layouts  7.87 us (10%)
  other arithmetic  1.34 us (2%)
    pallas_call x1, Pallas kernels, body(): pl.pallas_call(functools.partial(kernel, (nd, nv, full, ck, AQ, VB)), out...  66.1 us
    unnamed x2, local copies, waits for them, and re-layouts  7.17 us

profile of v1, /device:TPU:0, one launch (start us, length us, event | category | flops | bytes accessed | tf_op | source)
XLA Modules:
  0.0 76.0 jit_solution(3594912989168281817)
XLA Ops:
  0.6 0.7 convert_bitcast_fusion
  1.3 0.7 bitcast_convert_fusion
  2.0 0.1 tile.10
  2.1 0.6 pad.4.marks
  2.7 66.1 %shard_map.59 = (bf16[8,8,3584]{2,1,0:T(8,128)(2,1)}, bf16[768,3584]{1,0:T(8,128)(2,1)}) custom-call(bf16[64,3584]{1,0:T(8,128)(2,1)} %hidden.1, bf16[768,3584]{1,0:T(8,128)(2,1)} %embedding.1, f32[8,256]{1,0:T(8,128)} %pad.4.marks), custom_call_target="tpu_custom_call" | custom-call | tf_op jit(solution)/shard_map/pallas_call | solution.py:250
  68.8 1.8 %copy.8 = bf16[64,3584]{1,0:T(8,128)(2,1)} copy(bf16[64,3584]{1,0:T(8,128)(2,1)} %bitcast.6) | data formatting | bytes 917504
  70.6 5.4 %copy.9 = bf16[768,3584]{1,0:T(8,128)(2,1)} copy(bf16[768,3584]{1,0:T(8,128)(2,1)} %get-tuple-element.9) | data formatting | bytes 11010048
  (4 shorter events, 0.0 us)

commit v2 on v0

v2 whole, which is shorter than its diff:
```python
import functools

import jax
import jax.numpy as jnp
from jax import lax
from jax.experimental import pallas as pl
from jax.experimental.pallas import tpu as pltpu
from jax.sharding import PartitionSpec as P

soft_cap = 30.0
z_weight = 0.002
MESH = pl.DeviceIdType.MESH
VMEM_LIMIT = 45
f32, bf16 = jnp.float32, jnp.bfloat16


def kernel(cfg, hidden, embedding, targets, weights, hgrad, tgrad,
           hid, emb, tw, pd, pv, uT, eT, sT, sN, gF, sC, rC, sY, rY, bF, sX, rX, sZ, rZ, out,
           loc, tw_s, tw_r, hc_s, hc_r, hy_s, hy_r, hf_s, hf_r, pd_s, pd_r, pv_s, pv_r,
           c_s, c_r, y_s, y_r, x_s, x_r, z_s, z_r, az_s, az_r, ax_s, ax_r):
    nd, nv, full, ck, NH, VB, TC = cfg
    Y, Z = nd // 2, nv // 2
    rows, D = hidden.shape
    V = embedding.shape[0]
    K = D // ck
    part = rows // NH
    TH = nd * part
    d, v = lax.axis_index("dp"), lax.axis_index("vocab")
    c, y = lax.rem(d, 2), d // 2
    x, z = lax.rem(v, 2), v // 2
    dev = lambda dd, vv: dict(device_id=(dd, vv), device_id_type=MESH)
    core = dev(y * 2 + 1 - c, v)
    xdev = dev(d, z * 2 + 1 - x)
    ydev = lambda k: dev(lax.rem(y + k, Y) * 2 + c, v)
    zdev = lambda k: dev(d, lax.rem(z + k, Z) * 2 + x)
    ddev = lambda k: dev(lax.rem(d + k, nd), v)
    vdev = lambda k: dev(d, lax.rem(v + k, nv))
    rdma = lambda s, t, ss, rs, dv: pltpu.make_async_remote_copy(src_ref=s, dst_ref=t, send_sem=ss, recv_sem=rs, **dv)

    block = lambda dd, a: hid.at[pl.ds(pl.multiple_of(a * TH + dd * part, part), part)]
    loads = [pltpu.make_async_copy(hidden.at[pl.ds(a * part, part)], block(d, a), loc.at[a]) for a in range(NH)]
    load_e = pltpu.make_async_copy(embedding, emb, loc.at[NH])
    for copy in loads:
        copy.start()
    load_e.start()
    barrier = pltpu.get_barrier_semaphore()
    for k in range(1, nd):
        pl.semaphore_signal(barrier, inc=1, **ddev(k))
    for k in range(1, nv):
        pl.semaphore_signal(barrier, inc=1, **vdev(k))
    T = NH * TH
    at = lax.broadcasted_iota(jnp.int32, (rows, T), 1)
    own = lax.broadcasted_iota(jnp.int32, (rows, T), 0)
    place = jnp.where((own // part) * TH + d * part + lax.rem(own, part) == at, 1.0, 0.0)
    line = jnp.concatenate([weights[...], targets[...].astype(f32), jnp.zeros((6, rows), f32)], axis=0)
    tw[0] = jnp.dot(line, place, precision=lax.Precision.HIGHEST, preferred_element_type=f32)
    for copy in loads:
        copy.wait()
    pl.semaphore_wait(barrier, nd + nv - 2)

    sends = []

    def go(copy):
        copy.start()
        sends.append(copy)
        return copy

    hy = lambda a, k: rdma(block(d, a), block(d, a), hy_s.at[a, k - 1], hy_r.at[a, k - 1], ydev(k))
    hc = lambda a: rdma(block(d, a), block(d, a), hc_s.at[a], hc_r.at[a], core)

    def hf(a, k):
        there = block(lax.rem(y + Y - k, Y) * 2 + c, a)
        return rdma(there, there, hf_s.at[a, k - 1], hf_r.at[a, k - 1], core)

    twc = lambda k: rdma(tw.at[0], tw.at[k], tw_s.at[k - 1], tw_r.at[k - 1], ddev(k))
    for k in range(1, nd):
        go(twc(k))
    for a in range(NH):
        for k in range(1, Y):
            go(hy(a, k))
        go(hc(a))

    def forward(a):
        for k in range(1, Y):
            hy(a, k).wait_recv()
            go(hf(a, k))

    def arrived(a):
        hc(a).wait_recv()
        for k in range(1, Y):
            hf(a, k).wait_recv()

    def logits(a):
        pd[a, 0] = jnp.zeros_like(pd[a, 0])

        def step(b, carry):
            vb = pl.ds(pl.multiple_of(b * VB, VB), VB)
            lg = lax.dot_general(emb[vb, :], hid[a * TH:(a + 1) * TH, :], (((1,), (1,)), ((), ())), preferred_element_type=f32)
            u = jnp.tanh(lg * (1.0 / soft_cap))
            e = jnp.exp(soft_cap * u - soft_cap)
            uT[a, vb, :] = 1.0 - u * u
            eT[a, vb, :] = e
            pd[a, 0] += jnp.sum(e.reshape(VB // 8, 8, TH), axis=0)
            return carry

        lax.fori_loop(0, V // VB, step, 0)

    pdc = lambda a, k: rdma(pd.at[a, 0], pd.at[a, k], pd_s.at[a, k - 1], pd_r.at[a, k - 1], ddev(k))
    pvc = lambda a, k: rdma(pv.at[a, 0], pv.at[a, k], pv_s.at[a, k - 1], pv_r.at[a, k - 1], vdev(k))

    def sums_out(a):
        for k in range(1, nd):
            go(pdc(a, k))

    def sums_on(a):
        for k in range(1, nd):
            pdc(a, k).wait_recv()
        pv[a, 0] = jnp.sum(pd[a], axis=0)
        for k in range(1, nv):
            go(pvc(a, k))

    first = (d * nv + v) * V

    def scores(a):
        for k in range(1, nv):
            pvc(a, k).wait_recv()
        total = jnp.sum(jnp.sum(pv[a], axis=0), axis=0, keepdims=True)
        group = jnp.sum(tw[:, :, a * TH:(a + 1) * TH], axis=0)
        weight, target = group[0:1, :], group[1:2, :]
        factor = weight * (1.0 + 2.0 * z_weight * (soft_cap + jnp.log(total))) / total

        def step(b, carry):
            vb = pl.ds(pl.multiple_of(b * VB, VB), VB)
            cols = (first + b * VB + lax.broadcasted_iota(jnp.int32, (VB, TH), 0)).astype(f32)
            s = (factor * eT[a, vb, :] - jnp.where(cols == target, weight, 0.0)) * uT[a, vb, :]
            sT[vb, a * TH:(a + 1) * TH] = s.astype(bf16)
            sN[a * TH:(a + 1) * TH, vb] = s.T.astype(bf16)
            return carry

        lax.fori_loop(0, V // VB, step, 0)

    ccopy = lambda i: rdma(sC.at[i], rC.at[i], c_s.at[i], c_r.at[i], core)
    ycopy = lambda i, k: rdma(sY.at[i, k - 1], rY.at[i, k - 1], y_s.at[i, k - 1], y_r.at[i, k - 1], ydev(k))

    def core_unit(i):
        ccopy(i).wait()
        for k in range(1, Y):
            yy = lax.rem(y + k, Y)
            sY[i, k - 1] = (gF[i, yy * 2 + c] + rC[i, yy].astype(f32)).astype(bf16)
            ycopy(i, k).start()

    def partials(a):
        def step(j, carry):
            i = a * K + j
            g = jnp.dot(sN[a * TH:(a + 1) * TH, :], emb[:, pl.ds(pl.multiple_of(j * ck, ck), ck)], preferred_element_type=f32)
            gF[i] = g.reshape(nd, part, ck)
            for yy in range(Y):
                sC[i, yy] = gF[i, yy * 2 + 1 - c].astype(bf16)
            ccopy(i).start()

            @pl.when(j >= 2)
            def _():
                core_unit(i - 2)

            return carry

        lax.fori_loop(0, K, step, 0)
        for j in range(max(K - 2, 0), K):
            core_unit(a * K + j)

    forward(0)
    for k in range(1, nd):
        twc(k).wait_recv()
    arrived(0)
    load_e.wait()
    logits(0)
    sums_out(0)
    for a in range(1, NH):
        forward(a)
        sums_on(a - 1)
        arrived(a)
        logits(a)
        sums_out(a)
        scores(a - 1)
        sums_on(a)
        partials(a - 1)
    if NH == 1:
        sums_on(0)
    scores(NH - 1)
    partials(NH - 1)

    pieces = [(b, j) for b in range(V // VB) for j in range(D // TC)]

    def table(b, j):
        vb, cs = pl.ds(b * VB, VB), pl.ds(j * TC, TC)
        tgrad[vb, cs] = jnp.dot(sT[vb, :], hid[:, cs], preferred_element_type=f32).astype(bf16)

    U = NH * K

    def y_unit(i):
        acc = gF[i, y * 2 + c] + rC[i, y].astype(f32)
        for k in range(1, Y):
            ycopy(i, k).wait()
            acc = acc + rY[i, k - 1].astype(f32)
        return acc

    if not full:
        for piece in pieces:
            table(*piece)
        for i in range(U):
            a, j = i // K, i % K
            hgrad[a * part:(a + 1) * part, j * ck:(j + 1) * ck] = y_unit(i)
    else:
        h = part // 8
        gz = h // Z
        cx = ck // 2
        xcopy = lambda i: rdma(sX.at[i], rX.at[i], x_s.at[i], x_r.at[i], xdev)
        zcopy = lambda i, k: rdma(sZ.at[i, k - 1], rZ.at[i, k - 1], z_s.at[i, k - 1], z_r.at[i, k - 1], zdev(k))
        mycols = lambda i: pl.ds(pl.multiple_of((i % K) * ck + x * cx, cx), cx)
        mine = lambda i: out.at[pl.ds((i // K) * h + z * gz, gz), :, mycols(i)]
        half = lambda i: out.at[pl.ds((i // K) * h, h), :, mycols(i)]
        azcopy = lambda i, k: rdma(mine(i), mine(i), az_s.at[i, k - 1], az_r.at[i, k - 1], zdev(k))
        axcopy = lambda i: rdma(half(i), half(i), ax_s.at[i], ax_r.at[i], xdev)
        xsum = lambda i, zz: bF[i, x, pl.ds(zz * gz, gz)] + rX[i, pl.ds(zz * gz, gz)].astype(f32)

        def stage0(i):
            acc = y_unit(i).reshape(h, 8, ck)
            for xx in range(2):
                bF[i, xx] = acc[:, :, xx * cx:(xx + 1) * cx]
            sX[i] = bF[i, 1 - x].astype(bf16)
            xcopy(i).start()

        def stage1(i):
            xcopy(i).wait()
            for k in range(1, Z):
                sZ[i, k - 1] = xsum(i, lax.rem(z + k, Z)).astype(bf16)
                zcopy(i, k).start()

        def stage2(i):
            acc = xsum(i, z)
            for k in range(1, Z):
                zcopy(i, k).wait()
                acc = acc + rZ[i, k - 1].astype(f32)
            out[pl.ds((i // K) * h + z * gz, gz), :, mycols(i)] = acc.astype(bf16)
            for k in range(1, Z):
                azcopy(i, k).start()

        def stage3(i):
            for k in range(1, Z):
                azcopy(i, k).wait()
            axcopy(i).start()

        plan = [(stage0, 0), (stage1, 3), (stage2, 8), (stage3, 13)]
        for s in range(U + plan[-1][1]):
            for _ in range(2):
                if pieces:
                    table(*pieces.pop())
            for stage, lag in plan:
                if 0 <= s - lag < U:
                    stage(s - lag)
        for piece in pieces:
            table(*piece)
        for i in range(U):
            axcopy(i).wait()
        hgrad[...] = out[...]
    for copy in sends:
        copy.wait_send()


def body(hidden, embedding, targets, loss_weight):
    nd, nv = lax.axis_size("dp"), lax.axis_size("vocab")
    rows, D = hidden.shape
    V = embedding.shape[0]
    T = rows * nd
    Y, Z = nd // 2, nv // 2
    ck = next(s for s in (512, 256, D) if D % s == 0)
    TC = next(s for s in (896, 512, 256, 128, D) if D % s == 0)
    K = D // ck
    NH = 2
    VB = next(s for s in (256, 128, V) if V % s == 0)
    part = rows // NH
    TH = nd * part
    U = NH * K
    full = (part // 8) % Z == 0
    h = part // 8
    gz = max(h // Z, 1)
    cx = ck // 2
    Zs, Ys = max(Z - 1, 1), max(Y - 1, 1)
    VM = pltpu.VMEM
    dma = lambda *shape: pltpu.SemaphoreType.DMA(shape)
    scratch = [
        VM((T, D), bf16), VM((V, D), bf16), VM((nd, 8, T), f32), VM((NH, nd, 8, TH), f32), VM((NH, nv, 8, TH), f32),
        VM((NH, V, TH), f32), VM((NH, V, TH), f32), VM((V, T), bf16), VM((T, V), bf16),
        VM((U, nd, part, ck), f32), VM((U, Y, part, ck), bf16), VM((U, Y, part, ck), bf16),
        VM((U, Ys, part, ck), bf16), VM((U, Ys, part, ck), bf16),
        VM((U, 2, h, 8, cx), f32), VM((U, h, 8, cx), bf16), VM((U, h, 8, cx), bf16),
        VM((U, Zs, gz, 8, cx), bf16), VM((U, Zs, gz, 8, cx), bf16),
        VM((NH * h, 8, D), bf16),
        dma(NH + 1), dma(nd), dma(nd), dma(NH), dma(NH), dma(NH, Ys), dma(NH, Ys), dma(NH, Ys), dma(NH, Ys),
        dma(NH, nd), dma(NH, nd), dma(NH, nv), dma(NH, nv),
        dma(U), dma(U), dma(U, Ys), dma(U, Ys), dma(U), dma(U), dma(U, Zs), dma(U, Zs), dma(U, Zs), dma(U, Zs), dma(U), dma(U),
    ]
    hshape = jax.ShapeDtypeStruct((NH * h, 8, D), bf16) if full else jax.ShapeDtypeStruct((rows, D), f32)
    any_spec = pl.BlockSpec(memory_space=pltpu.HBM)
    vmem_spec = pl.BlockSpec(memory_space=pltpu.VMEM)
    hgrad, tgrad = pl.pallas_call(
        functools.partial(kernel, (nd, nv, full, ck, NH, VB, TC)),
        out_shape=(hshape, jax.ShapeDtypeStruct((V, D), bf16)),
        in_specs=[any_spec, any_spec, vmem_spec, vmem_spec],
        out_specs=(vmem_spec, vmem_spec),
        scratch_shapes=scratch,
        compiler_params=pltpu.CompilerParams(collective_id=0, has_side_effects=True, vmem_limit_bytes=VMEM_LIMIT * 1024 * 1024),
    )(hidden, embedding, targets.reshape(1, rows), loss_weight.astype(f32).reshape(1, rows))
    if full:
        return hgrad.reshape(rows, D), tgrad
    return lax.psum(hgrad, "vocab").astype(bf16), tgrad


def solution(mesh):
    return jax.shard_map(
        body,
        mesh=mesh,
        in_specs=(P("dp", None), P(("dp", "vocab"), None), P("dp"), P("dp")),
        out_specs=(P("dp", None), P(("dp", "vocab"), None)),
        check_vma=False,
    )
```

time: 183 us -> 64.9 us (0.35)
  blocking collectives: 102 us -> 0 us
  Pallas kernels: 0 us -> 58.5 us
  waiting for transfers between devices: 47.6 us -> 0 us
  matrix products: 15.4 us -> 0 us
  between operations: 14.7 us -> 0.64 us
  local copies, waits for them, and re-layouts: 2.97 us -> 4.89 us
    psum x2 -> x0, blocking collectives: 88.7 us -> none  [the longest x1 49.4 us: body(): hidden_grad = lax.psum(group_grad, 'vocab').astype(jnp.bfloat16)]
    pallas_call x0 -> x1, Pallas kernels: none -> 58.5 us  [body(): pl.pallas_call(functools.partial(kernel, (nd, nv, full, ck, NH, VB, TC)),...]
    reduce_scatter x1 -> x0, waiting for transfers between devices: 37.9 us -> none  [body(): lax.psum_scatter(jnp.dot(scores_grad, embedding, preferred_element_type=j...]
    dot_general x3 -> x0, matrix products: 15.4 us -> none  [the longest x1 6.28 us: body(): jnp.dot(scores_grad, embedding, preferred_element_type=jnp.float32)]
    unnamed x2 -> x0, blocking collectives: 12.8 us -> none
    all_gather x1 -> x0, waiting for transfers between devices: 9.04 us -> none  [body(): lax.all_gather(hidden, 'dp', axis=0, tiled=True)]
    unnamed x7 -> x6, local copies, waits for them, and re-layouts: 2.97 us -> 4.89 us
  transfers between devices with their start and end apart: 2 -> 0, of which waited for: 2 -> 0; matrix products, arithmetic and copies ran while one was open for 4% -> 0% of each run, Pallas kernels for 0% -> 0%
where the time goes in v2:
time: 64.9 us; the launch traced here: 64.7 us
  Pallas kernels  58.5 us (90%)
  local copies, waits for them, and re-layouts  4.89 us (8%)
  other arithmetic  0.66 us (1%)
    pallas_call x1, Pallas kernels, body(): pl.pallas_call(functools.partial(kernel, (nd, nv, full, ck, NH, VB, TC)),...  58.5 us
    unnamed x6, local copies, waits for them, and re-layouts  4.89 us

profile of v2, /device:TPU:0, one launch (start us, length us, event | category | flops | bytes accessed | tf_op | source)
XLA Modules:
  0.0 64.7 jit_solution(12616919480364430335)
XLA Ops:
  0.6 0.7 %bitcast_convert_fusion.weights = f32[1,64]{1,0:T(1,128)S(1)} fusion(bf16[64]{0:T(256)(128)(2,1)} %param.7), kind=kLoop, calls=%fused_computation | loop fusion | flops 64 | bytes 384 | tf_op jit(solution)/shard_map/reshape | solution.py:313
  1.3 0.0 copy-start
  1.3 1.0 %copy-done = bf16[64,3584]{1,0:T(8,128)(2,1)S(1)} copy-done((bf16[64,3584]{1,0:T(8,128)(2,1)S(1)}, bf16[64,3584]{1,0:T(8,128)(2,1)}, u32[]{:S(2)}) %copy-start) | copy-done | bytes 458776
  2.3 0.0 copy-start.1
  2.3 0.7 %copy-done.1 = s32[64]{0:T(128)S(1)} copy-done((s32[64]{0:T(128)S(1)}, s32[64]{0:T(128)}, u32[]{:S(2)}) %copy-start.1) | copy-done | bytes 280
  3.0 58.5 %shard_map.59 = (bf16[8,8,3584]{2,1,0:T(8,128)(2,1)S(1)}, bf16[768,3584]{1,0:T(8,128)(2,1)S(1)}) custom-call(bf16[64,3584]{1,0:T(8,128)(2,1)S(1)} %copy-done, bf16[768,3584]{1,0:T(8,128)(2,1)} %embedding.1, s32[1,64]{1,0:T(1,128)S(1)} %bitcast.6, f32[1,64]{1,0:T(1,128)S(1)} %bitcast_convert_fusion.weights), custom_call_target="tpu_custom_call" | custom-call | tf_op jit(solution)/shard_map/pallas_call | solution.py:306
  61.5 0.8 %copy.8 = bf16[64,3584]{1,0:T(8,128)(2,1)} copy(bf16[64,3584]{1,0:T(8,128)(2,1)S(1)} %bitcast.5) | data formatting | bytes 917504
  62.3 2.4 %copy.9 = bf16[768,3584]{1,0:T(8,128)(2,1)} copy(bf16[768,3584]{1,0:T(8,128)(2,1)S(1)} %get-tuple-element.9) | data formatting | bytes 11010048
Async XLA Ops:
  1.3 1.0 %copy-start = (bf16[64,3584]{1,0:T(8,128)(2,1)S(1)}, bf16[64,3584]{1,0:T(8,128)(2,1)}, u32[]{:S(2)}) copy-start(bf16[64,3584]{1,0:T(8,128)(2,1)} %hidden.1) | copy-start | bytes 1376260
  2.3 0.7 %copy-start.1 = (s32[64]{0:T(128)S(1)}, s32[64]{0:T(128)}, u32[]{:S(2)}) copy-start(s32[64]{0:T(128)} %param.6) | copy-start | bytes 772

commit v3 on v2

--- a/solution.py
+++ b/solution.py
@@ -250,14 +250,28 @@
                 azcopy(i, k).wait()
             axcopy(i).start()
 
-        plan = [(stage0, 0), (stage1, 3), (stage2, 8), (stage3, 13)]
-        for s in range(U + plan[-1][1]):
-            for _ in range(2):
+        def filler(count):
+            for _ in range(count):
                 if pieces:
-                    table(*pieces.pop())
-            for stage, lag in plan:
-                if 0 <= s - lag < U:
-                    stage(s - lag)
+                    table(*pieces.pop(0))
+
+        def run(stage, a):
+            for i in range(a * K, (a + 1) * K):
+                stage(i)
+
+        third = -(-len(pieces) // 3)
+        run(stage0, 0)
+        filler(third)
+        for a in range(NH):
+            run(stage1, a)
+            filler(third)
+            if a + 1 < NH:
+                run(stage0, a + 1)
+                filler(third)
+            if a > 0:
+                run(stage3, a - 1)
+            run(stage2, a)
+        run(stage3, NH - 1)
         for piece in pieces:
             table(*piece)
         for i in range(U):
@@ -273,7 +287,7 @@
     V = embedding.shape[0]
     T = rows * nd
     Y, Z = nd // 2, nv // 2
-    ck = next(s for s in (512, 256, D) if D % s == 0)
+    ck = next(s for s in (1792, 512, 256, D) if D % s == 0)
     TC = next(s for s in (896, 512, 256, 128, D) if D % s == 0)
     K = D // ck
     NH = 2

time: 64.9 us -> 60.2 us (0.928)
  Pallas kernels: 58.5 us -> 53.8 us
    pallas_call x1, Pallas kernels: 58.5 us -> 53.8 us  [body(): pl.pallas_call(functools.partial(kernel, (nd, nv, full, ck, NH, VB, TC)),...]
where the time goes in v3:
time: 60.2 us; the launch traced here: 60 us
  Pallas kernels  53.8 us (89%)
  local copies, waits for them, and re-layouts  4.89 us (8%)
  other arithmetic  0.66 us (1%)
  between operations  0.64 us (1%)
    pallas_call x1, Pallas kernels, body(): pl.pallas_call(functools.partial(kernel, (nd, nv, full, ck, NH, VB, TC)),...  53.8 us
    unnamed x6, local copies, waits for them, and re-layouts  4.89 us

profile of v3, /device:TPU:0, one launch (start us, length us, event | category | flops | bytes accessed | tf_op | source)
XLA Modules:
  0.0 60.0 jit_solution(11113715525525904238)
XLA Ops:
  0.6 0.7 %bitcast_convert_fusion.weights = f32[1,64]{1,0:T(1,128)S(1)} fusion(bf16[64]{0:T(256)(128)(2,1)} %param.7), kind=kLoop, calls=%fused_computation | loop fusion | flops 64 | bytes 384 | tf_op jit(solution)/shard_map/reshape | solution.py:327
  1.3 0.0 copy-start
  1.3 1.0 %copy-done = bf16[64,3584]{1,0:T(8,128)(2,1)S(1)} copy-done((bf16[64,3584]{1,0:T(8,128)(2,1)S(1)}, bf16[64,3584]{1,0:T(8,128)(2,1)}, u32[]{:S(2)}) %copy-start) | copy-done | bytes 458776
  2.3 0.0 copy-start.1
  2.3 0.7 %copy-done.1 = s32[64]{0:T(128)S(1)} copy-done((s32[64]{0:T(128)S(1)}, s32[64]{0:T(128)}, u32[]{:S(2)}) %copy-start.1) | copy-done | bytes 280
  3.0 53.8 %shard_map.59 = (bf16[8,8,3584]{2,1,0:T(8,128)(2,1)S(1)}, bf16[768,3584]{1,0:T(8,128)(2,1)S(1)}) custom-call(bf16[64,3584]{1,0:T(8,128)(2,1)S(1)} %copy-done, bf16[768,3584]{1,0:T(8,128)(2,1)} %embedding.1, s32[1,64]{1,0:T(1,128)S(1)} %bitcast.6, f32[1,64]{1,0:T(1,128)S(1)} %bitcast_convert_fusion.weights), custom_call_target="tpu_custom_call" | custom-call | tf_op jit(solution)/shard_map/pallas_call | solution.py:320
  56.8 0.8 %copy.8 = bf16[64,3584]{1,0:T(8,128)(2,1)} copy(bf16[64,3584]{1,0:T(8,128)(2,1)S(1)} %bitcast.5) | data formatting | bytes 917504
  57.6 2.4 %copy.9 = bf16[768,3584]{1,0:T(8,128)(2,1)} copy(bf16[768,3584]{1,0:T(8,128)(2,1)S(1)} %get-tuple-element.9) | data formatting | bytes 11010048
Async XLA Ops:
  1.3 1.0 %copy-start = (bf16[64,3584]{1,0:T(8,128)(2,1)S(1)}, bf16[64,3584]{1,0:T(8,128)(2,1)}, u32[]{:S(2)}) copy-start(bf16[64,3584]{1,0:T(8,128)(2,1)} %hidden.1) | copy-start | bytes 1376260
  2.3 0.7 %copy-start.1 = (s32[64]{0:T(128)S(1)}, s32[64]{0:T(128)}, u32[]{:S(2)}) copy-start(s32[64]{0:T(128)} %param.6) | copy-start | bytes 772
